TPU v7x, 16 devices: a whole 2x2x2 slice. The times are simulated.
16 devices in a mesh: etp: 4 (over z, y), ep: 4 (over x, core).
Axes of the slice: x: 2, y: 2, z: 2, core: 2. Of those that a mesh axis runs over, the one named last changes fastest.
Arguments:
- hidden: bfloat16 [65536, 256], P(('ep', 'etp'))
- w_router: float32 [256, 64], replicated
- expert_ids: int32 [65536, 2], P(('ep', 'etp'))
- d_out: bfloat16 [65536, 256], P(('ep', 'etp'))
- w_gate: bfloat16 [64, 256, 1024], P('ep', None, 'etp')
- w_up: bfloat16 [64, 256, 1024], P('ep', None, 'etp')
- w_down: bfloat16 [64, 1024, 256], P('ep', 'etp')
Outputs:
- output 1: bfloat16 [65536, 256], P(('ep', 'etp'))
- output 2: bfloat16 [65536, 256], P(('ep', 'etp'))
- output 3: float32 [256, 64], replicated
- output 4: float32 [], replicated
- output 5: float32 [64, 256, 1024], P('ep', None, 'etp')
- output 6: float32 [64, 256, 1024], P('ep', None, 'etp')
- output 7: float32 [64, 1024, 256], P('ep', 'etp')
All inputs are finite; a program needn't handle non-finite values.
Results may differ from a plain program's by a relative error of at most 0.00894483.
Values are sent between devices in bfloat16 or wider.
A program may use at most 1 GiB of HBM per device.

v0:
```python
import functools
import jax
import jax.numpy as jnp
from jax import lax
from jax.experimental import pallas as pl
from jax.experimental.pallas import tpu as pltpu
from jax.sharding import PartitionSpec as P


AUX_COEF = 0.01
OUT_SCALE = 2.0
GROUP = 128
F32 = jnp.float32
BF16 = jnp.bfloat16
HI = lax.Precision.HIGHEST
MESH = pl.DeviceIdType.MESH
NT = (((1,), (1,)), ((), ()))
TN = (((0,), (0,)), ((), ()))


def dot(a, b, dims=(((1,), (0,)), ((), ())), precision=None):
    return lax.dot_general(a, b, dims, precision=precision, preferred_element_type=F32)


def flip(index, mask, bits):
    total = 0
    for bit in range(bits):
        total = total + ((index // 2**bit + mask // 2**bit) % 2) * 2**bit
    return total


def route_kernel(per_expert, hidden_ref, wr_ref, ids_ref, pos_ref, gate_ref, prob_ref, stat_ref):
    n_experts = wr_ref.shape[0]
    rows = hidden_ref.shape[0]
    block = min(512, rows)
    iota_e = lax.broadcasted_iota(jnp.int32, (n_experts, block), 0)
    upper = (lax.broadcasted_iota(jnp.int32, (block, block), 0) < lax.broadcasted_iota(jnp.int32, (block, block), 1)).astype(BF16)
    ones = jnp.ones((8, block), BF16)
    ones_f = jnp.ones((8, block), F32)
    wr = wr_ref[...]
    wr_hi = wr.astype(BF16)
    rest = wr - wr_hi.astype(F32)
    wr_mid = rest.astype(BF16)
    wr_lo = (rest - wr_mid.astype(F32)).astype(BF16)
    gate_ref[...] = jnp.zeros_like(gate_ref)
    carry = jnp.zeros((n_experts, 1), F32)
    counts = jnp.zeros((8, n_experts), F32)
    probs = jnp.zeros((8, n_experts), F32)
    for i in range(rows // block):
        cols = pl.ds(i * block, block)
        h = hidden_ref[cols, :]
        z = dot(wr_lo, h, NT) + dot(wr_mid, h, NT) + dot(wr_hi, h, NT)
        e = jnp.exp(z - jnp.max(z, axis=0, keepdims=True))
        p = e / jnp.sum(e, axis=0, keepdims=True)
        prob_ref[:, cols] = p
        id0 = ids_ref[0:1, cols]
        id1 = ids_ref[1:2, cols]
        hit0 = iota_e == id0
        hit1 = iota_e == id1
        p0 = jnp.sum(jnp.where(hit0, p, 0.0), axis=0, keepdims=True)
        p1 = jnp.sum(jnp.where(hit1, p, 0.0), axis=0, keepdims=True)
        den = p0 + p1
        gate_ref[0:1, cols] = p0 / den
        gate_ref[1:2, cols] = p1 / den
        hits = jnp.where(hit0 | hit1, 1.0, 0.0).astype(F32)
        hits_b = hits.astype(BF16)
        rank = dot(hits_b, upper) + carry
        r0 = jnp.sum(jnp.where(hit0, rank, 0.0), axis=0, keepdims=True)
        r1 = jnp.sum(jnp.where(hit1, rank, 0.0), axis=0, keepdims=True)
        pos_ref[0:1, cols] = id0 * per_expert + r0.astype(jnp.int32)
        pos_ref[1:2, cols] = id1 * per_expert + r1.astype(jnp.int32)
        carry = carry + jnp.sum(hits, axis=1, keepdims=True)
        counts = counts + dot(ones, hits_b, NT)
        probs = probs + dot(ones_f, p, NT, HI)
    stat_ref[:, 0:n_experts] = counts
    stat_ref[:, n_experts:2 * n_experts] = probs


def scatter_kernel(steps, pos_ref, gate_ref, hidden_ref, dout_ref, send_ref, first_ref, second_ref, slots_ref):
    step = pl.program_id(0)
    block, d = hidden_ref.shape
    tile = send_ref.shape[0]

    @pl.when(step < steps)
    def _():
        x = hidden_ref[...].astype(F32)
        m = OUT_SCALE * dout_ref[...].astype(F32)
        g = gate_ref[...].T
        x = x.reshape(block // 8, 8, d)
        first_ref[:, :, 0:d] = x
        first_ref[:, :, d:2 * d] = (g[:, 0:1] * m).reshape(block // 8, 8, d)
        second_ref[:, :, 0:d] = x
        second_ref[:, :, d:2 * d] = (g[:, 1:2] * m).reshape(block // 8, 8, d)

        def group(c, _):
            for i in range(GROUP):
                for k, ref in enumerate((first_ref, second_ref)):
                    q = pos_ref[step * (block // GROUP) + c, k, i]
                    slots_ref[pl.ds(q, 1), :] = ref[c * (GROUP // 8) + i // 8, i % 8:i % 8 + 1, :]
            return 0

        lax.fori_loop(0, block // GROUP, group, 0)

    @pl.when(step >= steps)
    def _():
        start = pl.multiple_of((step - steps) * tile, tile)
        send_ref[...] = slots_ref[pl.ds(start, tile), :].astype(BF16)


def expert_kernel(
    ep, etp, capacity, send_ref, stat_ref, *refs,
):
    own, near, twin, refs = refs[0:3], (refs[3:6], refs[6:9]), (refs[9:12], refs[12:15]), refs[15:]
    back_ref = refs[0]
    mine, onward_in, onward_out = (refs[1:4], refs[4:7]), refs[7:9], refs[9:11]
    tab_out_ref, x_ref, w13_ref, w2f_ref, ga13_ref, ga2_ref, ga2t_ref, twin_ref, xm_ref, u_ref, dab_ref, tab_ref = refs[11:23]
    stat_send, stat_recv, w_recv, relay_send, relay_recv, x_send, x_recv, back_send, back_recv, g_done, g_send, g_recv = refs[23:]
    n_dev = ep * etp
    n_slots, n_src, rows, _ = x_ref.shape
    per = n_slots // 2
    ring = ga13_ref.shape[0]
    d = w2f_ref.shape[2]
    ff = w2f_ref.shape[1]
    part = ff // etp
    bits = n_dev.bit_length() - 1
    src_bits = n_src.bit_length() - 1
    me_o = lax.axis_index("ep")
    me_t = lax.axis_index("etp")
    me = me_o * etp + me_t
    z = me_t // 2
    y = me_t % 2
    t_y = flip(me_t, 1, 2)
    t_z = flip(me_t, 2, 2)
    t_yz = flip(me_t, 3, 2)

    def pick(kind, first, second):
        return first + kind * (second - first)

    def place(kind, w):
        return pick(kind, w * 2 + y, z * 2 + w)

    def remote(src, dst, send, recv, o, t):
        pltpu.make_async_remote_copy(src_ref=src, dst_ref=dst, send_sem=send, recv_sem=recv, device_id={"ep": o, "etp": t}, device_id_type=MESH).start()

    def wait_bytes(ref, sem):
        pltpu.make_async_copy(ref, ref, sem).wait()

    barrier = pltpu.get_barrier_semaphore()

    def hello(i, _):
        peer = (me + i) % n_dev
        pl.semaphore_signal(barrier, inc=1, device_id={"ep": peer // etp, "etp": peer % etp}, device_id_type=MESH)
        return 0

    lax.fori_loop(1, n_dev, hello, 0)
    pl.semaphore_wait(barrier, n_dev - 1)

    def lanes(offset, t):
        return pl.ds(pl.multiple_of(offset + t * part, part), part)

    def places(kind, t):
        group = slice(kind * per, (kind + 1) * per)
        return w13_ref.at[group, :, lanes(0, t)], w13_ref.at[group, :, lanes(ff, t)], w2f_ref.at[group, lanes(0, t), :]

    relays, loads = [], []
    for kind in range(2):
        beside, across = (t_z, t_y) if kind == 0 else (t_y, t_z)
        start = pick(kind, z * per, (2 + y) * per)
        for w in range(3):
            n = kind * 3 + w
            relays.append(pltpu.make_async_remote_copy(
                src_ref=near[kind][w], dst_ref=places(kind, beside)[w], send_sem=relay_send.at[n], recv_sem=relay_recv.at[n],
                device_id={"ep": me_o, "etp": across}, device_id_type=MESH,
            ))
            for ref, t in ((own[w].at[pl.ds(start, per)], me_t), (near[kind][w], beside), (twin[kind][w], across)):
                loads.append(pltpu.make_async_copy(ref, places(kind, t)[w], w_recv.at[len(loads)]))
    for copy in relays + loads:
        copy.start()

    def send_stats(i, _):
        peer = flip(me, (i * 11) % n_dev, bits)
        remote(stat_ref, tab_ref.at[me], stat_send, stat_recv, peer // etp, peer % etp)
        return 0

    lax.fori_loop(1, n_dev, send_stats, 0)
    tab_ref[me] = stat_ref[...]

    def expert_of(o, kind, w, k):
        return o * (4 * per) + kind * (2 * per) + w * per + k

    def send_slot(i, _):
        kind, k = i % 2, i // 2
        here = me_o * 2 + pick(kind, z, y)
        pltpu.make_async_copy(send_ref.at[expert_of(me_o, kind, pick(kind, z, y), k)], x_ref.at[i, here], x_recv.at[i]).start()

        def tokens(m, _):
            there = flip(here, (m * 3) % n_src, src_bits)
            o, w = there // 2, there % 2
            remote(send_ref.at[expert_of(o, kind, w, k)], x_ref.at[i, here], x_send, x_recv.at[i], o, place(kind, w))
            return 0

        lax.fori_loop(1, n_src, tokens, 0)
        return 0

    lax.fori_loop(0, n_slots, send_slot, 0)

    wait_bytes(tab_ref.at[0:n_dev - 1], stat_recv)
    tab_out_ref[...] = tab_ref[...]
    table = tab_ref[:, 0, :]
    shape = table.shape
    below = (lax.broadcasted_iota(jnp.int32, (n_dev, n_dev), 1) < lax.broadcasted_iota(jnp.int32, (n_dev, n_dev), 0)).astype(F32)
    keep = jnp.minimum(table, capacity - dot(below, table, precision=HI))
    src_iota = lax.broadcasted_iota(jnp.int32, shape, 0)
    lane_iota = lax.broadcasted_iota(jnp.int32, shape, 1)
    row_iota = lax.broadcasted_iota(jnp.int32, (rows, 2 * d), 0).astype(F32)

    for copy in loads:
        copy.wait()
    for copy in relays:
        copy.wait_recv()

    def do_slot(i, _):
        kind, k = i % 2, i // 2
        at = kind * per + k
        r = i % ring
        v = pick(kind, z, y)
        expert = expert_of(me_o, kind, v, k)

        @pl.when(i >= ring)
        def _():
            wait_bytes(twin_ref.at[0], g_send.at[r])

        wait_bytes(x_ref.at[i], x_recv.at[i])
        ga13_ref[r] = jnp.zeros((d, 2 * ff), F32)
        ga2t_ref[...] = jnp.zeros((d, ff), F32)

        def give_back(b):
            o = flip(me_o, b, 2)
            for w in range(2):
                away = (o - me_o) * (o - me_o) + (w - v) * (w - v)

                @pl.when(away == 0)
                def _():
                    pltpu.make_async_copy(x_ref.at[i, o * 2 + w], back_ref.at[expert], back_recv).start()

                @pl.when(away != 0)
                def _():
                    remote(x_ref.at[i, o * 2 + w], back_ref.at[expert], back_send, back_recv, o, place(kind, w))

        def do_block(b, _):
            o = flip(me_o, b, 2)
            for w in range(2):
                limit = jnp.sum(jnp.where((src_iota == o * etp + place(kind, w)) & (lane_iota == expert), keep, 0.0), keepdims=True)
                full = x_ref[i, o * 2 + w].astype(F32)
                xm_ref[w * rows:(w + 1) * rows, :] = jnp.where(row_iota < limit, full, 0.0).astype(BF16)
            x = xm_ref[:, 0:d]
            c = xm_ref[:, d:2 * d]
            for q in range(etp):
                here = slice(q * part, (q + 1) * part)
                there = slice(ff + q * part, ff + (q + 1) * part)
                a = dot(x, w13_ref[at, :, here])
                up = dot(x, w13_ref[at, :, there])
                du = dot(c, w2f_ref[at, here, :], NT)
                sig = jax.nn.sigmoid(a)
                silu = a * sig
                u_ref[:, here] = (silu * up).astype(BF16)
                dab_ref[:, here] = (du * up * sig * (1.0 + a * (1.0 - sig))).astype(BF16)
                dab_ref[:, there] = (du * silu).astype(BF16)
            out = dot(u_ref[...], w2f_ref[at]).astype(BF16)
            dx = dot(dab_ref[...], w13_ref[at], NT).astype(BF16)
            for w in range(2):
                x_ref[i, o * 2 + w, :, 0:d] = out[w * rows:(w + 1) * rows]
                x_ref[i, o * 2 + w, :, d:2 * d] = dx[w * rows:(w + 1) * rows]
            ga13_ref[r] += dot(x, dab_ref[...], TN)
            ga2t_ref[...] += dot(c, u_ref[...], TN)

            @pl.when(b > 0)
            def _():
                give_back(b - 1)

            return 0

        lax.fori_loop(0, ep, do_block, 0)
        ga2_ref[r] = ga2t_ref[...].T
        give_back(ep - 1)

        for one in range(2):
            @pl.when(kind == one)
            def _():
                across = t_y if one == 0 else t_z
                for w in range(3):
                    remote(parts(r, across)[w], twin_ref.at[i, w], g_send.at[r], g_recv.at[i], me_o, across)
                    remote(parts(r, t_yz)[w], twin_ref.at[i, 3 + w], g_send.at[r], g_recv.at[i], me_o, across)

        @pl.when(i >= 2)
        def _():
            add_twin(i - 2)

        return 0

    def parts(r, t):
        return ga13_ref.at[r, :, lanes(0, t)], ga13_ref.at[r, :, lanes(ff, t)], ga2_ref.at[r, lanes(0, t), :]

    def add_twin(i):
        kind, k = i % 2, i // 2
        r = i % ring
        wait_bytes(twin_ref.at[i], g_recv.at[i])
        for one in range(2):
            @pl.when(kind == one)
            def _():
                beside = t_z if one == 0 else t_y
                for w in range(3):
                    twin_ref[i, w] += parts(r, me_t)[w][...]
                    twin_ref[i, 3 + w] += parts(r, beside)[w][...]
                for w in range(3):
                    pltpu.make_async_copy(twin_ref.at[i, w], mine[one][w].at[k], g_done).start()
                    onward = onward_in[one].at[w * per + k] if w < 2 else onward_out[one].at[k]
                    pltpu.make_async_copy(twin_ref.at[i, 3 + w], onward, g_done).start()

    lax.fori_loop(0, n_slots, do_slot, 0)
    lax.fori_loop(n_slots - 2, n_slots, lambda i, _: (add_twin(i), 0)[1], 0)

    others = (n_src - 1) * n_slots
    wait_bytes(tab_ref.at[0:n_dev - 1], stat_send)
    for copy in relays:
        copy.wait_send()
    wait_bytes(send_ref.at[0:others], x_send)
    wait_bytes(send_ref.at[0:others], back_send)
    for r in range(ring):
        wait_bytes(twin_ref.at[0], g_send.at[r])
    wait_bytes(back_ref, back_recv)
    wait_bytes(twin_ref, g_done)


def combine_kernel(
    n_tokens, chunk,
    pos_ref, back_ref, tab_ref, wr_ref, hidden_ref, dout_ref, ids_ref, gate_ref, prob_ref,
    out_ref, dh_ref, dwr_ref, aux_ref,
    rows_ref, stage_ref, first_ref, second_ref, sem,
):
    step = pl.program_id(0)
    block, d = hidden_ref.shape
    n_experts = wr_ref.shape[0]
    n_chunks = rows_ref.shape[0] // chunk

    totals = jnp.sum(tab_ref[:, 0:1, :], axis=0)
    frac = totals[:, 0:n_experts] / (2 * n_tokens)

    def fetch(i, slot):
        start = pl.multiple_of(i * chunk, chunk)
        return pltpu.make_async_copy(back_ref.at[pl.ds(start, chunk), :], stage_ref.at[slot], sem.at[slot])

    @pl.when(step == 0)
    def _():
        fetch(0, 0).start()

        def body(i, _):
            slot = i % 2

            @pl.when(i + 1 < n_chunks)
            def _():
                fetch(i + 1, 1 - slot).start()

            fetch(i, slot).wait()
            rows_ref[pl.ds(pl.multiple_of(i * chunk, chunk), chunk), :] = stage_ref[slot].astype(F32)
            return 0

        lax.fori_loop(0, n_chunks, body, 0)
        dwr_ref[...] = jnp.zeros_like(dwr_ref)
        mean_prob = totals[:, n_experts:2 * n_experts] / n_tokens
        aux_ref[0, 0] = AUX_COEF * n_experts * jnp.sum(frac * mean_prob)

    def group(c, _):
        for i in range(GROUP):
            for k, ref in enumerate((first_ref, second_ref)):
                q = pos_ref[step * (block // GROUP) + c, k, i]
                ref[c * (GROUP // 8) + i // 8, i % 8:i % 8 + 1, :] = rows_ref[pl.ds(q, 1), :]
        return 0

    lax.fori_loop(0, block // GROUP, group, 0)

    h = hidden_ref[...].astype(F32)
    dy = dout_ref[...].astype(F32)
    m = OUT_SCALE * dy
    y0 = first_ref[:, :, 0:d].reshape(block, d)
    y1 = second_ref[:, :, 0:d].reshape(block, d)
    dx = (first_ref[:, :, d:2 * d] + second_ref[:, :, d:2 * d]).reshape(block, d)
    g = gate_ref[...].T
    out_ref[...] = (h + OUT_SCALE * (g[:, 0:1] * y0 + g[:, 1:2] * y1)).astype(BF16)

    ones = jnp.ones((8, d), F32)
    dg0 = dot(ones, m * y0, NT, HI)[0:1]
    dg1 = dot(ones, m * y1, NT, HI)[0:1]
    p = prob_ref[...]
    iota_e = lax.broadcasted_iota(jnp.int32, p.shape, 0)
    hit0 = iota_e == ids_ref[0:1, :]
    hit1 = iota_e == ids_ref[1:2, :]
    den = jnp.sum(jnp.where(hit0 | hit1, p, 0.0), axis=0, keepdims=True)
    mean = gate_ref[0:1, :] * dg0 + gate_ref[1:2, :] * dg1
    eye = lax.broadcasted_iota(jnp.int32, (n_experts, n_experts), 0) == lax.broadcasted_iota(jnp.int32, (n_experts, n_experts), 1)
    ct = (AUX_COEF * n_experts / n_tokens) * jnp.sum(jnp.where(eye, frac, 0.0), axis=1, keepdims=True)
    dp = jnp.where(hit0, (dg0 - mean) / den, 0.0) + jnp.where(hit1, (dg1 - mean) / den, 0.0) + ct
    dz = p * (dp - jnp.sum(p * dp, axis=0, keepdims=True))
    dwr_ref[...] += dot(dz, h, precision=HI)
    dh_ref[...] = (dy + dx + dot(dz, wr_ref[...], TN, HI)).astype(BF16)


def sum_kernel(ep, etp, part_ref, out_ref, box_ref, mine_ref, all_ref, send1, recv1, send2, recv2):
    n_dev = ep * etp
    across = part_ref.shape[1] // 128
    me = lax.axis_index("ep") * etp + lax.axis_index("etp")

    def where_is(peer):
        return {"ep": peer // etp, "etp": peer % etp}

    def tile(ref, i):
        return ref.at[pl.ds(pl.multiple_of((i // across) * 8, 8), 8), pl.ds(pl.multiple_of((i % across) * 128, 128), 128)]

    def wait_bytes(ref, sem):
        pltpu.make_async_copy(ref, ref, sem).wait()

    barrier = pltpu.get_barrier_semaphore()

    def hello(i, _):
        pl.semaphore_signal(barrier, inc=1, device_id=where_is((me + i) % n_dev), device_id_type=MESH)
        return 0

    lax.fori_loop(1, n_dev, hello, 0)
    pl.semaphore_wait(barrier, n_dev - 1)

    def first(i, _):
        peer = (me + i) % n_dev
        pltpu.make_async_remote_copy(tile(part_ref, peer), box_ref.at[me], send1, recv1, device_id=where_is(peer), device_id_type=MESH).start()
        return 0

    lax.fori_loop(1, n_dev, first, 0)
    pltpu.make_async_copy(tile(part_ref, me), box_ref.at[me], recv1).start()
    wait_bytes(box_ref, recv1)
    mine_ref[...] = jnp.sum(box_ref[...], axis=0)

    def second(i, _):
        peer = (me + i) % n_dev
        pltpu.make_async_remote_copy(mine_ref, all_ref.at[me], send2, recv2, device_id=where_is(peer), device_id_type=MESH).start()
        return 0

    lax.fori_loop(1, n_dev, second, 0)
    all_ref[me] = mine_ref[...]
    wait_bytes(all_ref.at[0:n_dev - 1], recv2)
    for i in range(n_dev):
        out_ref[(i // across) * 8:(i // across) * 8 + 8, (i % across) * 128:(i % across) * 128 + 128] = all_ref[i]
    wait_bytes(box_ref.at[0:n_dev - 1], send1)
    wait_bytes(all_ref.at[0:n_dev - 1], send2)


def starts_of(per):
    me_t = lax.axis_index("etp")
    z, y = me_t // 2, me_t % 2
    return (z * per, (2 + y) * per), ((1 - z) * per, (3 - y) * per)


def place_kernel(per, plan, *refs):
    parts, outs = refs[:-6], refs[-6:-3]
    stage_ref, in_sem, out_sem = refs[-3:]
    starts = starts_of(per)
    loads, stores = [], []
    for i, (ref, row, out, kind, came) in enumerate(plan):
        loads.append(pltpu.make_async_copy(parts[ref].at[row:row + per], stage_ref.at[i], in_sem.at[i]))
        stores.append(pltpu.make_async_copy(stage_ref.at[i], outs[out].at[pl.ds(starts[came][kind], per)], out_sem.at[i]))
    for load in loads:
        load.start()
    for load, store in zip(loads, stores):
        load.wait()
        store.start()
    for store in stores:
        store.wait()


def place_last_kernel(per, first_ref, second_ref, _, out_ref, sem):
    starts = starts_of(per)[1]
    copies = [pltpu.make_async_copy(ref, out_ref.at[pl.ds(starts[i], per)], sem.at[i]) for i, ref in enumerate((first_ref, second_ref))]
    for copy in copies:
        copy.start()
    for copy in copies:
        copy.wait()


def solution(mesh):
    ep_size = mesh.shape["ep"]
    etp_size = mesh.shape["etp"]
    n_dev = ep_size * etp_size
    all_axes = ("ep", "etp")
    tok_spec = P(all_axes, None)
    gate_spec = P("ep", None, "etp")
    down_spec = P("ep", "etp", None)

    def layer(hidden, w_router, expert_ids, d_out, w_gate, w_up, w_down):
        rows, d = hidden.shape
        n_experts = w_router.shape[1]
        n_tokens = rows * n_dev
        capacity = (5 * n_tokens + 2 * n_experts - 1) // (2 * n_experts)
        per_expert = 7 * rows // (2 * n_experts)
        n_slots = n_experts // n_dev
        local_experts, _, part = w_gate.shape
        ff = part * etp_size
        all_slots = n_experts * per_expert
        assert etp_size == 4 and ep_size == 4
        me_t = lax.axis_index("etp")
        z, y = me_t // 2, me_t % 2
        per = n_experts // ep_size // 4
        swap_y = [(t, t ^ 1) for t in range(4)]
        swap_z = [(t, t ^ 2) for t in range(4)]

        weights = w_gate, w_up, w_down

        def parts_at(w, start):
            return lax.dynamic_slice_in_dim(w, start, per)

        near, twin = ([], []), ([], [])
        for w in weights:
            near[0].append(lax.ppermute(parts_at(w, (1 - z) * per), "etp", swap_z))
            near[1].append(lax.ppermute(parts_at(w, (3 - y) * per), "etp", swap_y))
            twin[0].append(lax.ppermute(parts_at(w, z * per), "etp", swap_y))
            twin[1].append(lax.ppermute(parts_at(w, (2 + y) * per), "etp", swap_z))
        ids_t = expert_ids.T
        wr_t = w_router.T

        vmem = pl.BlockSpec(memory_space=pltpu.VMEM)
        smem = pl.BlockSpec(memory_space=pltpu.SMEM)
        anywhere = pl.BlockSpec(memory_space=pl.ANY)
        big = 60 * 1024 * 1024

        pos, gates, probs, stats = pl.pallas_call(
            functools.partial(route_kernel, per_expert),
            out_shape=(
                jax.ShapeDtypeStruct((2, rows), jnp.int32),
                jax.ShapeDtypeStruct((8, rows), F32),
                jax.ShapeDtypeStruct((n_experts, rows), F32),
                jax.ShapeDtypeStruct((8, 2 * n_experts), F32),
            ),
            in_specs=[vmem] * 3,
            out_specs=(vmem,) * 4,
            cost_estimate=pl.CostEstimate(flops=5_000_000_000, bytes_accessed=4_000_000, transcendentals=0),
            name="route",
        )(hidden, wr_t, ids_t)

        block = min(512, rows)
        steps = rows // block
        pos = pos.reshape(2, rows // GROUP, GROUP).transpose(1, 0, 2)
        tile = n_slots * per_expert
        tiles = all_slots // tile
        send = pl.pallas_call(
            functools.partial(scatter_kernel, steps),
            out_shape=jax.ShapeDtypeStruct((all_slots, 2 * d), BF16),
            grid=(steps + tiles,),
            in_specs=[
                smem,
                pl.BlockSpec((8, block), lambda i: (0, jnp.minimum(i, steps - 1))),
                pl.BlockSpec((block, d), lambda i: (jnp.minimum(i, steps - 1), 0)),
                pl.BlockSpec((block, d), lambda i: (jnp.minimum(i, steps - 1), 0)),
            ],
            out_specs=pl.BlockSpec((tile, 2 * d), lambda i: (jnp.maximum(i - steps, 0), 0)),
            scratch_shapes=[pltpu.VMEM((block // 8, 8, 2 * d), F32)] * 2 + [pltpu.VMEM((all_slots, 2 * d), F32)],
            compiler_params=pltpu.CompilerParams(vmem_limit_bytes=big),
            cost_estimate=pl.CostEstimate(flops=50_000_000_000, bytes_accessed=20_000_000, transcendentals=0),
            name="scatter",
        )(pos, gates, hidden, d_out)
        send = send.reshape(n_experts, per_expert, 2 * d)

        dma = pltpu.SemaphoreType.DMA
        assert part == d
        slots = 2 * per
        sources = n_dev // 2
        ring = 3
        results = (jax.ShapeDtypeStruct((local_experts, d, part), F32),) * 3
        back, *rest = pl.pallas_call(
            functools.partial(expert_kernel, ep_size, etp_size, float(capacity)),
            out_shape=(
                jax.ShapeDtypeStruct((n_experts, per_expert, 2 * d), BF16),
                *(jax.ShapeDtypeStruct((per, d, part), F32),) * 6,
                *(jax.ShapeDtypeStruct((2 * per, d, part), F32),) * 2,
                *(jax.ShapeDtypeStruct((per, d, part), F32),) * 2,
                jax.ShapeDtypeStruct((n_dev, 8, 2 * n_experts), F32),
            ),
            in_specs=[anywhere, vmem] + [anywhere] * 15,
            out_specs=(anywhere,) * 11 + (vmem,),
            scratch_shapes=[
                pltpu.VMEM((slots, sources, per_expert, 2 * d), BF16),
                pltpu.VMEM((slots, d, 2 * ff), BF16),
                pltpu.VMEM((slots, ff, d), BF16),
                pltpu.VMEM((ring, d, 2 * ff), F32),
                pltpu.VMEM((ring, ff, d), F32),
                pltpu.VMEM((d, ff), F32),
                pltpu.VMEM((slots, 6, d, part), F32),
                pltpu.VMEM((2 * per_expert, 2 * d), BF16),
                pltpu.VMEM((2 * per_expert, ff), BF16),
                pltpu.VMEM((2 * per_expert, 2 * ff), BF16),
                pltpu.VMEM((n_dev, 8, 2 * n_experts), F32),
                dma, dma, dma((18,)), dma((6,)), dma((6,)), dma, dma((slots,)), dma, dma, dma, dma((ring,)), dma((slots,)),
            ],
            cost_estimate=pl.CostEstimate(flops=300_000_000_000, bytes_accessed=60_000_000, transcendentals=0),
            compiler_params=pltpu.CompilerParams(collective_id=0, has_side_effects=True, vmem_limit_bytes=big),
            name="experts",
        )(send, stats, *weights, *near[0], *near[1], *twin[0], *twin[1])
        table = rest[-1]
        mine = rest[0:6]
        came_in = [lax.ppermute(part_in, "etp", swap) for part_in, swap in zip(rest[6:8], (swap_z, swap_y))]
        came_out = [lax.ppermute(part_out, "etp", swap) for part_out, swap in zip(rest[8:10], (swap_z, swap_y))]

        cols = lambda n: pl.BlockSpec((n, block), lambda i: (0, i))
        tok = pl.BlockSpec((block, d), lambda i: (i, 0))
        output, d_hidden, dwr_part, aux_loss = pl.pallas_call(
            functools.partial(combine_kernel, n_tokens, tile),
            out_shape=(
                jax.ShapeDtypeStruct((rows, d), BF16),
                jax.ShapeDtypeStruct((rows, d), BF16),
                jax.ShapeDtypeStruct((n_experts, d), F32),
                jax.ShapeDtypeStruct((1, 1), F32),
            ),
            grid=(steps,),
            in_specs=[smem, anywhere, vmem, vmem, tok, tok, cols(2), cols(8), cols(n_experts)],
            out_specs=(tok, tok, pl.BlockSpec((n_experts, d), lambda i: (0, 0)), smem),
            scratch_shapes=[
                pltpu.VMEM((all_slots, 2 * d), F32),
                pltpu.VMEM((2, tile, 2 * d), BF16),
                pltpu.VMEM((block // 8, 8, 2 * d), F32),
                pltpu.VMEM((block // 8, 8, 2 * d), F32),
                dma((2,)),
            ],
            compiler_params=pltpu.CompilerParams(vmem_limit_bytes=big),
            cost_estimate=pl.CostEstimate(flops=60_000_000_000, bytes_accessed=30_000_000, transcendentals=0),
            name="combine",
        )(pos, back.reshape(all_slots, 2 * d), table, wr_t, hidden, d_out, ids_t, gates, probs)

        plan = [(kind * 3 + w, 0, w, kind, 0) for w in (2, 0, 1) for kind in range(2)]
        plan += [(6 + kind, w * per, w, kind, 1) for w in range(2) for kind in range(2)]
        half = pl.pallas_call(
            functools.partial(place_kernel, per, plan),
            out_shape=results,
            in_specs=[anywhere] * 8,
            out_specs=(anywhere,) * 3,
            scratch_shapes=[pltpu.VMEM((len(plan), per, d, part), F32), dma((len(plan),)), dma((len(plan),))],
            cost_estimate=pl.CostEstimate(flops=10_000_000_000, bytes_accessed=20_000_000, transcendentals=0),
            compiler_params=pltpu.CompilerParams(vmem_limit_bytes=big),
            name="place",
        )(*mine, *came_in)
        dwr_part, *half = lax.optimization_barrier((dwr_part, *half))
        dwr = pl.pallas_call(
            functools.partial(sum_kernel, ep_size, etp_size),
            out_shape=jax.ShapeDtypeStruct((n_experts, d), F32),
            in_specs=[vmem],
            out_specs=vmem,
            scratch_shapes=[
                pltpu.VMEM((n_dev, 8, 128), F32), pltpu.VMEM((8, 128), F32), pltpu.VMEM((n_dev, 8, 128), F32),
                dma, dma, dma, dma,
            ],
            compiler_params=pltpu.CompilerParams(collective_id=1, has_side_effects=True),
            cost_estimate=pl.CostEstimate(flops=10_000_000_000, bytes_accessed=100_000, transcendentals=0),
            name="sum_router",
        )(dwr_part)
        g_gate, g_up = half[0:2]
        g_down = pl.pallas_call(
            functools.partial(place_last_kernel, per),
            out_shape=results[2],
            in_specs=[vmem, vmem, anywhere],
            out_specs=anywhere,
            input_output_aliases={2: 0},
            scratch_shapes=[dma((2,))],
            compiler_params=pltpu.CompilerParams(vmem_limit_bytes=8 * 1024 * 1024),
            name="place_last",
        )(*came_out, half[2])
        return output, d_hidden, dwr.T, aux_loss.reshape(()), g_gate, g_up, g_down

    return jax.shard_map(layer, mesh=mesh, in_specs=(tok_spec, P(), tok_spec, tok_spec, gate_spec, gate_spec, down_spec), out_specs=(tok_spec, tok_spec, P(), P(), gate_spec, gate_spec, down_spec), check_vma=False)
```

profile of v0, /device:TPU:0, one launch (start us, length us, event | category | flops | bytes accessed | tf_op | source)
XLA Modules:
  0.0 511.4 jit_solution(7453070188689562883)
XLA Ops:
  0.7 0.0 copy-start
  0.7 2.8 constant_dynamic-slice_fusion.2
  3.5 3.3 collective-permute-start.9
  6.7 1.5 collective-permute-start.6
  8.3 0.5 collective-permute-start.3
  8.8 0.0 copy-start.1
  8.8 0.0 collective-permute-start
  8.8 0.0 copy-done
  8.8 1.1 constant_dynamic-slice_fusion.1
  9.9 2.0 collective-permute-start.10
  11.9 7.6 %collective-permute-done.9.refs_12_ = bf16[4,256,256]{2,1,0:T(8,128)(2,1)S(1)} collective-permute-done((bf16[4,256,256]{2,1,0:T(8,128)(2,1)S(1)}, bf16[4,256,256]{2,1,0:T(8,128)(2,1)S(1)}, u32[]{:S(2)}, u32[]{:S(2)}) %collective-permute-start.9) | collective-permute-done | bytes 524320 | tf_op jit(solution)/shard_map/ppermute | solution.py:523
  19.5 0.0 copy-start.3
  19.5 2.0 collective-permute-start.7
  21.5 0.1 collective-permute-done.6.refs_9_
  21.5 0.0 copy-start.4
  21.5 1.5 collective-permute-start.4
  23.1 0.0 copy-done.1
  23.1 0.2 constant_dynamic-slice_fusion
  23.3 0.0 copy-done.3
  23.3 0.0 copy-done.4
  23.3 6.4 %route.1 = (s32[2,4096]{1,0:T(2,128)}, f32[8,4096]{1,0:T(8,128)}, f32[64,4096]{1,0:T(8,128)}, f32[8,128]{1,0:T(8,128)}) custom-call(bf16[4096,256]{1,0:T(8,128)(2,1)} %hidden_ref.5, f32[64,256]{1,0:T(8,128)} %bitcast.10, s32[2,4096]{1,0:T(2,128)} %bitcast.12), custom_call_target="tpu_custom_call" | custom-call | flops 5000000000 | bytes 4000000 | tf_op jit(solution)/shard_map/route/pallas_call | solution.py:532
  29.7 3.2 collective-permute-done.3.refs_6_
  32.9 0.0 collective-permute-start.1
  32.9 0.0 collective-permute-done.refs_3_
  32.9 2.0 collective-permute-start.11
  34.9 7.2 %collective-permute-done.10.refs_13_ = bf16[4,256,256]{2,1,0:T(8,128)(2,1)} collective-permute-done((bf16[4,256,256]{2,1,0:T(8,128)(2,1)}, bf16[4,256,256]{2,1,0:T(8,128)(2,1)}, u32[]{:S(2)}, u32[]{:S(2)}) %collective-permute-start.10) | collective-permute-done | bytes 524320 | tf_op jit(solution)/shard_map/ppermute | solution.py:523
  42.1 2.0 collective-permute-start.8
  44.1 0.1 collective-permute-done.7.refs_10_
  44.1 1.5 collective-permute-start.5
  45.6 9.7 %collective-permute-done.4.refs_7_ = bf16[4,256,256]{2,1,0:T(8,128)(2,1)} collective-permute-done((bf16[4,256,256]{2,1,0:T(8,128)(2,1)S(1)}, bf16[4,256,256]{2,1,0:T(8,128)(2,1)}, u32[]{:S(2)}, u32[]{:S(2)}) %collective-permute-start.4) | collective-permute-done | bytes 524320 | tf_op jit(solution)/shard_map/ppermute | solution.py:521
  55.4 0.0 collective-permute-start.2
  55.4 28.8 %scatter.1 = bf16[14336,512]{1,0:T(8,128)(2,1)} custom-call(s32[32,2,128]{2,1,0:T(2,128)} %bitcast.16, f32[8,4096]{1,0:T(8,128)} %get-tuple-element.35.gate_ref, bf16[4096,256]{1,0:T(8,128)(2,1)} %hidden_ref.5, bf16[4096,256]{1,0:T(8,128)(2,1)} %dout_ref.3), custom_call_target="tpu_custom_call" | custom-call | flops 49999998976 | bytes 20000000 | tf_op jit(solution)/shard_map/scatter/pallas_call | solution.py:551
  84.2 0.0 collective-permute-done.1.refs_4_
  84.2 0.0 copy-start.5
  84.2 0.0 collective-permute-done.11.refs_14_
  84.2 0.0 collective-permute-done.8.refs_11_
  84.2 0.0 collective-permute-done.5.refs_8_
  84.2 0.0 collective-permute-done.2.refs_5_
  84.2 0.0 copy-start.6
  84.2 0.7 copy-done.5
  85.0 0.2 copy-done.6
  85.1 335.2 %experts.1 = (bf16[64,224,512]{2,1,0:T(8,128)(2,1)}, f32[4,256,256]{2,1,0:T(8,128)}, f32[4,256,256]{2,1,0:T(8,128)}, f32[4,256,256]{2,1,0:T(8,128)}, f32[4,256,2...) custom-call(bf16[64,224,512]{2,1,0:T(8,128)(2,1)} %bitcast.15, ...), custom_call_target="tpu_custom_call" | custom-call | flops 299999985664 | bytes 60000000 | tf_op jit(solution)/shard_map/experts/pallas_call | solution.py:575
  420.3 1.5 collective-permute-start.14
  421.8 0.6 collective-permute-start.15
  422.4 0.6 collective-permute-start.12
  423.0 1.4 collective-permute-start.13
  424.4 44.9 %combine.1 = (bf16[4096,256]{1,0:T(8,128)(2,1)}, bf16[4096,256]{1,0:T(8,128)(2,1)}, f32[64,256]{1,0:T(8,128)}, f32[1,1]{1,0:T(1,128)}) custom-call(s32[32,2,128]{2,1,0:T(2,128)} %bitcast.17, bf16[14336,512]{1,0:T(8,128)(2,1)} %bitcast.14, f32[16,8,128]{2,1,0:T(8,128)} %get-tuple-element.38.tab_ref, f32[64,256]{1,0:T(8,128)} %bitcast.11, ...), custom_call_target="tpu_custom_call" | custom-call | flops 60000002048 | bytes 30000000 | tf_op jit(solution)/shard_map/combine/pallas_call | solution.py:611
  469.3 21.2 %collective-permute-done.12.refs_6_ = f32[8,256,256]{2,1,0:T(8,128)} collective-permute-done((f32[8,256,256]{2,1,0:T(8,128)}, f32[8,256,256]{2,1,0:T(8,128)}, u32[]{:S(2)}, u32[]{:S(2)}) %collective-permute-start.12) | collective-permute-done | bytes 2097184 | tf_op jit(solution)/shard_map/ppermute | solution.py:606
  490.5 1.1 collective-permute-done.13.refs_7_
  491.6 8.2 %place.1 = (f32[16,256,256]{2,1,0:T(8,128)}, f32[16,256,256]{2,1,0:T(8,128)}, f32[16,256,256]{2,1,0:T(8,128)}) custom-call(f32[4,256,256]{2,1,0:T(8,128)} %get-tuple-element.43.refs_0_, f32[4,256,256]{2,1,0:T(8,128)} %get-tuple-element.44.refs_1_, f32[4,256,256]{2,1,0:T(8,128)} %get-tuple-element.45.refs_2_, f32[4,256,256]{2,1,0:T(8,128)} %get-tuple-element.46.refs_3_, ...), custom_call_target="tpu_custom_call" | custom-call | flops 10000000000 | bytes 20000000 | tf_op jit(solution)/shard_map/place/pallas_call | solution.py:636
  499.8 9.6 %sum_router.1 = f32[64,256]{1,0:T(8,128)} custom-call(f32[64,256]{1,0:T(8,128)} %get-tuple-element.54.part_ref), custom_call_target="tpu_custom_call" | custom-call | flops 10000000000 | bytes 100000 | tf_op jit(solution)/shard_map/sum_router/pallas_call | solution.py:647
  509.4 0.0 copy-start.2
  509.4 0.0 collective-permute-done.14.first_ref
  509.4 0.0 collective-permute-done.15.second_ref
  509.4 1.4 place_last.1
  510.8 0.0 copy-done.2
  510.8 0.6 copy.17
Async XLA Ops:
  0.7 8.1 %copy-start = (bf16[16,256,256]{2,1,0:T(8,128)(2,1)S(1)}, bf16[16,256,256]{2,1,0:T(8,128)(2,1)}, u32[]{:S(2)}) copy-start(bf16[16,256,256]{2,1,0:T(8,128)(2,1)} %refs_1_.1) | copy-start | bytes 6291460
  3.5 16.1 %collective-permute-start.9 = (bf16[4,256,256]{2,1,0:T(8,128)(2,1)S(1)}, bf16[4,256,256]{2,1,0:T(8,128)(2,1)S(1)}, u32[]{:S(2)}, u32[]{:S(2)}) collective-permute-start(bf16[4,256,256]{2,1,0:T(8,128)(2,1)S(1)} %get-tuple-element.69), channel_id=1, source_target_pairs={{0,8},{4,12},{8,0},{12,4},{1,9},{5,13},{9,1},{13,5},{2,10},{6,14},... | collective-permute-start | bytes 1572872 | tf_op jit(solution)/shard_map/ppermute | solution.py:523
  6.7 14.8 %collective-permute-start.6 = (bf16[4,256,256]{2,1,0:T(8,128)(2,1)S(1)}, bf16[4,256,256]{2,1,0:T(8,128)(2,1)S(1)}, u32[]{:S(2)}, u32[]{:S(2)}) collective-permute-start(bf16[4,256,256]{2,1,0:T(8,128)(2,1)S(1)} %get-tuple-element.70), channel_id=1, source_target_pairs={{0,4},{4,0},{8,12},{12,8},{1,5},{5,1},{9,13},{13,9},{2,6},{6,2},{1... | collective-permute-start | bytes 1572872 | tf_op jit(solution)/shard_map/ppermute | solution.py:522
  8.3 24.6 %collective-permute-start.3 = (bf16[4,256,256]{2,1,0:T(8,128)(2,1)}, bf16[4,256,256]{2,1,0:T(8,128)(2,1)}, u32[]{:S(2)}, u32[]{:S(2)}) collective-permute-start(bf16[4,256,256]{2,1,0:T(8,128)(2,1)} %get-tuple-element.71), channel_id=1, source_target_pairs={{0,4},{4,0},{8,12},{12,8},{1,5},{5,1},{9,13},{13,9},{2,6},{6,2},{1... | collective-permute-start | bytes 1572872 | tf_op jit(solution)/shard_map/ppermute | solution.py:521
  8.8 14.3 %copy-start.1 = (bf16[16,256,256]{2,1,0:T(8,128)(2,1)S(1)}, bf16[16,256,256]{2,1,0:T(8,128)(2,1)}, u32[]{:S(2)}) copy-start(bf16[16,256,256]{2,1,0:T(8,128)(2,1)} %refs_2_.1) | copy-start | bytes 6291460
  8.8 24.1 %collective-permute-start = (bf16[4,256,256]{2,1,0:T(8,128)(2,1)}, bf16[4,256,256]{2,1,0:T(8,128)(2,1)}, u32[]{:S(2)}, u32[]{:S(2)}) collective-permute-start(bf16[4,256,256]{2,1,0:T(8,128)(2,1)} %get-tuple-element.72), channel_id=1, source_target_pairs={{0,8},{4,12},{8,0},{12,4},{1,9},{5,13},{9,1},{13,5},{2,10},{6,14},... | collective-permute-start | bytes 1572872 | tf_op jit(solution)/shard_map/ppermute | solution.py:520
  9.9 32.2 %collective-permute-start.10 = (bf16[4,256,256]{2,1,0:T(8,128)(2,1)}, bf16[4,256,256]{2,1,0:T(8,128)(2,1)}, u32[]{:S(2)}, u32[]{:S(2)}) collective-permute-start(bf16[4,256,256]{2,1,0:T(8,128)(2,1)} %get-tuple-element.65), channel_id=1, source_target_pairs={{0,8},{4,12},{8,0},{12,4},{1,9},{5,13},{9,1},{13,5},{2,10},{6,14},... | collective-permute-start | bytes 1572872 | tf_op jit(solution)/shard_map/ppermute | solution.py:523
  19.5 3.7 copy-start.3
  19.5 24.6 %collective-permute-start.7 = (bf16[4,256,256]{2,1,0:T(8,128)(2,1)}, bf16[4,256,256]{2,1,0:T(8,128)(2,1)}, u32[]{:S(2)}, u32[]{:S(2)}) collective-permute-start(bf16[4,256,256]{2,1,0:T(8,128)(2,1)} %get-tuple-element.66), channel_id=1, source_target_pairs={{0,4},{4,0},{8,12},{12,8},{1,5},{5,1},{9,13},{13,9},{2,6},{6,2},{1... | collective-permute-start | bytes 1572872 | tf_op jit(solution)/shard_map/ppermute | solution.py:522
  21.5 1.7 copy-start.4
  21.5 33.8 %collective-permute-start.4 = (bf16[4,256,256]{2,1,0:T(8,128)(2,1)S(1)}, bf16[4,256,256]{2,1,0:T(8,128)(2,1)}, u32[]{:S(2)}, u32[]{:S(2)}) collective-permute-start(bf16[4,256,256]{2,1,0:T(8,128)(2,1)S(1)} %get-tuple-element.67), channel_id=1, source_target_pairs={{0,4},{4,0},{8,12},{12,8},{1,5},{5,1},{9,13},{13,9},{2,6},{6,2},{1... | collective-permute-start | bytes 1572872 | tf_op jit(solution)/shard_map/ppermute | solution.py:521
  32.9 51.3 %collective-permute-start.1 = (bf16[4,256,256]{2,1,0:T(8,128)(2,1)S(1)}, bf16[4,256,256]{2,1,0:T(8,128)(2,1)S(1)}, u32[]{:S(2)}, u32[]{:S(2)}) collective-permute-start(bf16[4,256,256]{2,1,0:T(8,128)(2,1)S(1)} %get-tuple-element.68), channel_id=1, source_target_pairs={{0,8},{4,12},{8,0},{12,4},{1,9},{5,13},{9,1},{13,5},{2,10},{6,14},... | collective-permute-start | bytes 1572872 | tf_op jit(solution)/shard_map/ppermute | solution.py:520
  32.9 51.3 %collective-permute-start.11 = (bf16[4,256,256]{2,1,0:T(8,128)(2,1)S(1)}, bf16[4,256,256]{2,1,0:T(8,128)(2,1)}, u32[]{:S(2)}, u32[]{:S(2)}) collective-permute-start(bf16[4,256,256]{2,1,0:T(8,128)(2,1)S(1)} %get-tuple-element.61), channel_id=1, source_target_pairs={{0,8},{4,12},{8,0},{12,4},{1,9},{5,13},{9,1},{13,5},{2,10},{6,14},... | collective-permute-start | bytes 1572872 | tf_op jit(solution)/shard_map/ppermute | solution.py:523
  42.1 42.1 %collective-permute-start.8 = (bf16[4,256,256]{2,1,0:T(8,128)(2,1)S(1)}, bf16[4,256,256]{2,1,0:T(8,128)(2,1)}, u32[]{:S(2)}, u32[]{:S(2)}) collective-permute-start(bf16[4,256,256]{2,1,0:T(8,128)(2,1)S(1)} %get-tuple-element.62), channel_id=1, source_target_pairs={{0,4},{4,0},{8,12},{12,8},{1,5},{5,1},{9,13},{13,9},{2,6},{6,2},{1... | collective-permute-start | bytes 1572872 | tf_op jit(solution)/shard_map/ppermute | solution.py:522
  44.1 40.1 %collective-permute-start.5 = (bf16[4,256,256]{2,1,0:T(8,128)(2,1)S(1)}, bf16[4,256,256]{2,1,0:T(8,128)(2,1)}, u32[]{:S(2)}, u32[]{:S(2)}) collective-permute-start(bf16[4,256,256]{2,1,0:T(8,128)(2,1)S(1)} %get-tuple-element.63), channel_id=1, source_target_pairs={{0,4},{4,0},{8,12},{12,8},{1,5},{5,1},{9,13},{13,9},{2,6},{6,2},{1... | collective-permute-start | bytes 1572872 | tf_op jit(solution)/shard_map/ppermute | solution.py:521
  55.4 28.9 %collective-permute-start.2 = (bf16[4,256,256]{2,1,0:T(8,128)(2,1)S(1)}, bf16[4,256,256]{2,1,0:T(8,128)(2,1)S(1)}, u32[]{:S(2)}, u32[]{:S(2)}) collective-permute-start(bf16[4,256,256]{2,1,0:T(8,128)(2,1)S(1)} %get-tuple-element.64), channel_id=1, source_target_pairs={{0,8},{4,12},{8,0},{12,4},{1,9},{5,13},{9,1},{13,5},{2,10},{6,14},... | collective-permute-start | bytes 1572872 | tf_op jit(solution)/shard_map/ppermute | solution.py:520
  84.2 0.8 copy-start.5
  84.2 0.9 copy-start.6
  420.3 89.1 %collective-permute-start.14 = (f32[4,256,256]{2,1,0:T(8,128)}, f32[4,256,256]{2,1,0:T(8,128)S(1)}, u32[]{:S(2)}, u32[]{:S(2)}) collective-permute-start(f32[4,256,256]{2,1,0:T(8,128)} %get-tuple-element.58), channel_id=1, source_target_pairs={{0,8},{4,12},{8,0},{12,4},{1,9},{5,13},{9,1},{13,5},{2,10},{6,14},... | collective-permute-start | bytes 3145736 | tf_op jit(solution)/shard_map/ppermute | solution.py:607
  421.8 87.6 %collective-permute-start.15 = (f32[4,256,256]{2,1,0:T(8,128)}, f32[4,256,256]{2,1,0:T(8,128)S(1)}, u32[]{:S(2)}, u32[]{:S(2)}) collective-permute-start(f32[4,256,256]{2,1,0:T(8,128)} %get-tuple-element.59), channel_id=1, source_target_pairs={{0,4},{4,0},{8,12},{12,8},{1,5},{5,1},{9,13},{13,9},{2,6},{6,2},{1... | collective-permute-start | bytes 3145736 | tf_op jit(solution)/shard_map/ppermute | solution.py:607
  422.4 68.1 %collective-permute-start.12 = (f32[8,256,256]{2,1,0:T(8,128)}, f32[8,256,256]{2,1,0:T(8,128)}, u32[]{:S(2)}, u32[]{:S(2)}) collective-permute-start(f32[8,256,256]{2,1,0:T(8,128)} %get-tuple-element.49), channel_id=1, source_target_pairs={{0,8},{4,12},{8,0},{12,4},{1,9},{5,13},{9,1},{13,5},{2,10},{6,14},... | collective-permute-start | bytes 6291464 | tf_op jit(solution)/shard_map/ppermute | solution.py:606
  423.0 68.6 %collective-permute-start.13 = (f32[8,256,256]{2,1,0:T(8,128)}, f32[8,256,256]{2,1,0:T(8,128)}, u32[]{:S(2)}, u32[]{:S(2)}) collective-permute-start(f32[8,256,256]{2,1,0:T(8,128)} %get-tuple-element.50), channel_id=1, source_target_pairs={{0,4},{4,0},{8,12},{12,8},{1,5},{5,1},{9,13},{13,9},{2,6},{6,2},{1... | collective-permute-start | bytes 6291464 | tf_op jit(solution)/shard_map/ppermute | solution.py:606
  509.4 1.4 copy-start.2
where the time goes:
time: 512 us; the launch traced here: 511 us
  Pallas kernels  434 us (85%)
  waiting for transfers between devices  50 us (10%)
  starting transfers between devices  20.4 us (4%)
  local copies, waits for them, and re-layouts  5.66 us (1%)
    pallas_call x1, Pallas kernels, layer(): pl.pallas_call(functools.partial(expert_kernel, ep_size, etp_size, float(...  335 us
    pallas_call x1, Pallas kernels, layer(): pl.pallas_call(functools.partial(combine_kernel, n_tokens, tile), out_sha...  44.9 us
    pallas_call x1, Pallas kernels, layer(): pl.pallas_call(functools.partial(scatter_kernel, steps), out_shape=jax.Sh...  28.8 us
    ppermute x2, waiting for transfers between devices, layer(): lax.ppermute(part_in, 'etp', swap)  22.2 us
    ppermute x3, waiting for transfers between devices, layer(): twin[1].append(lax.ppermute(parts_at(w, (2 + y) * per), 'etp', swap_z))  14.8 us
    ppermute x3, waiting for transfers between devices, layer(): near[1].append(lax.ppermute(parts_at(w, (3 - y) * per), 'etp', swap_y))  12.9 us
  transfers between devices with their start and end apart: 16, of which 8 were waited for; matrix products, arithmetic and copies ran while one was open for 0% of the time, Pallas kernels for 19%

commit v1 on v0

--- a/solution.py
+++ b/solution.py
@@ -194,7 +194,7 @@
         pltpu.make_async_copy(send_ref.at[expert_of(me_o, kind, pick(kind, z, y), k)], x_ref.at[i, here], x_recv.at[i]).start()
 
         def tokens(m, _):
-            there = flip(here, (m * 3) % n_src, src_bits)
+            there = flip(here, (m * 5) % n_src, src_bits)
             o, w = there // 2, there % 2
             remote(send_ref.at[expert_of(o, kind, w, k)], x_ref.at[i, here], x_send, x_recv.at[i], o, place(kind, w))
             return 0
@@ -517,8 +517,11 @@
 
         near, twin = ([], []), ([], [])
         for w in weights:
-            near[0].append(lax.ppermute(parts_at(w, (1 - z) * per), "etp", swap_z))
-            near[1].append(lax.ppermute(parts_at(w, (3 - y) * per), "etp", swap_y))
+            first = [parts_at(w, (1 - z) * per), parts_at(w, (3 - y) * per)]
+            if w is w_gate:
+                *first, w = lax.optimization_barrier((*first, w))
+            near[0].append(lax.ppermute(first[0], "etp", swap_z))
+            near[1].append(lax.ppermute(first[1], "etp", swap_y))
             twin[0].append(lax.ppermute(parts_at(w, z * per), "etp", swap_y))
             twin[1].append(lax.ppermute(parts_at(w, (2 + y) * per), "etp", swap_z))
         ids_t = expert_ids.T

time: 512 us -> 511 us (level)
    ppermute x6, starting transfers between devices: 3.55 us -> 9.55 us  [the longest x3 5.31 us: layer(): near[0].append(lax.ppermute(first[0], 'etp', swap_z))]
    ppermute x3, waiting for transfers between devices: 14.8 us -> 9.28 us  [layer(): twin[1].append(lax.ppermute(parts_at(w, (2 + y) * per), 'etp', swap_z))]
    ppermute x3, starting transfers between devices: 7.32 us -> 2.12 us  [layer(): twin[1].append(lax.ppermute(parts_at(w, (2 + y) * per), 'etp', swap_z))]
  transfers between devices with their start and end apart: 16 -> 16, of which waited for: 8 -> 6; matrix products, arithmetic and copies ran while one was open for 0% -> 1% of each run, Pallas kernels for 19% -> 19%
where the time goes in v1:
time: 511 us
  Pallas kernels  435 us (85%)
  waiting for transfers between devices  48.1 us (9%)
  starting transfers between devices  19.7 us (4%)
  local copies, waits for them, and re-layouts  7.59 us (1%)
    pallas_call x1, Pallas kernels, layer(): pl.pallas_call(functools.partial(expert_kernel, ep_size, etp_size, float(...  335 us
    pallas_call x1, Pallas kernels, layer(): pl.pallas_call(functools.partial(combine_kernel, n_tokens, tile), out_sha...  44.9 us
    pallas_call x1, Pallas kernels, layer(): pl.pallas_call(functools.partial(scatter_kernel, steps), out_shape=jax.Sh...  28.8 us
    ppermute x2, waiting for transfers between devices, layer(): lax.ppermute(part_in, 'etp', swap)  22.2 us
  transfers between devices with their start and end apart: 16, of which 6 were waited for; matrix products, arithmetic and copies ran while one was open for 1% of the time, Pallas kernels for 19%

profile of v1, /device:TPU:0, one launch (start us, length us, event | category | flops | bytes accessed | tf_op | source)
XLA Modules:
  0.0 510.9 jit_solution(8985040276203137982)
XLA Ops:
  0.6 0.0 copy-start
  0.7 2.2 constant_dynamic-slice_fusion.10
  2.9 3.3 collective-permute-start
  6.2 1.5 collective-permute-start.3
  7.7 0.0 copy-done
  7.7 0.0 copy-start.1
  7.7 0.9 constant_dynamic-slice_fusion.2
  8.5 0.4 collective-permute-start.9
  9.0 0.0 copy-start.2
  9.0 0.1 collective-permute-start.6
  9.1 0.4 copy-done.1
  9.5 1.4 constant_dynamic-slice_fusion.1
  10.8 1.6 collective-permute-start.10
  12.4 6.8 %collective-permute-done.refs_3_ = bf16[4,256,256]{2,1,0:T(8,128)(2,1)} collective-permute-done((bf16[4,256,256]{2,1,0:T(8,128)(2,1)}, bf16[4,256,256]{2,1,0:T(8,128)(2,1)}, u32[]{:S(2)}, u32[]{:S(2)}) %collective-permute-start) | collective-permute-done | bytes 524320 | tf_op jit(solution)/shard_map/ppermute | solution.py:523
  19.2 2.0 collective-permute-start.7
  21.2 0.0 collective-permute-done.3.refs_6_
  21.2 1.4 collective-permute-start.4
  22.6 0.0 copy-done.2
  22.6 1.2 constant_dynamic-slice_fusion
  23.8 0.0 copy-start.3
  23.8 0.0 copy-start.6
  23.8 0.0 copy-start.5
  23.8 0.0 copy-start.4
  23.8 6.6 %route.1 = (s32[2,4096]{1,0:T(2,128)}, f32[8,4096]{1,0:T(8,128)}, f32[64,4096]{1,0:T(8,128)}, f32[8,128]{1,0:T(8,128)}) custom-call(bf16[4096,256]{1,0:T(8,128)(2,1)} %hidden_ref.5, f32[64,256]{1,0:T(8,128)} %bitcast.10, s32[2,4096]{1,0:T(2,128)} %bitcast.12), custom_call_target="tpu_custom_call" | custom-call | flops 5000000000 | bytes 4000000 | tf_op jit(solution)/shard_map/route/pallas_call | solution.py:535
  30.4 0.1 collective-permute-done.9.refs_12_
  30.5 0.0 copy-done.3
  30.5 2.0 collective-permute-start.1
  32.5 0.0 collective-permute-done.6.refs_9_
  32.5 0.0 copy-done.6
  32.5 0.0 collective-permute-start.11
  32.6 9.2 %collective-permute-done.10.refs_13_ = bf16[4,256,256]{2,1,0:T(8,128)(2,1)} collective-permute-done((bf16[4,256,256]{2,1,0:T(8,128)(2,1)}, bf16[4,256,256]{2,1,0:T(8,128)(2,1)}, u32[]{:S(2)}, u32[]{:S(2)}) %collective-permute-start.10) | collective-permute-done | bytes 524320 | tf_op jit(solution)/shard_map/ppermute | solution.py:526
  41.7 0.0 copy-done.5
  41.7 2.0 collective-permute-start.8
  43.7 0.0 collective-permute-done.7.refs_10_
  43.7 0.0 copy-done.4
  43.7 1.4 collective-permute-start.5
  45.1 9.7 %collective-permute-done.4.refs_7_ = bf16[4,256,256]{2,1,0:T(8,128)(2,1)} collective-permute-done((bf16[4,256,256]{2,1,0:T(8,128)(2,1)}, bf16[4,256,256]{2,1,0:T(8,128)(2,1)}, u32[]{:S(2)}, u32[]{:S(2)}) %collective-permute-start.4) | collective-permute-done | bytes 524320 | tf_op jit(solution)/shard_map/ppermute | solution.py:524
  54.8 0.0 collective-permute-start.2
  54.8 28.8 %scatter.1 = bf16[14336,512]{1,0:T(8,128)(2,1)} custom-call(s32[32,2,128]{2,1,0:T(2,128)} %bitcast.16, f32[8,4096]{1,0:T(8,128)} %get-tuple-element.38.gate_ref, bf16[4096,256]{1,0:T(8,128)(2,1)} %hidden_ref.5, bf16[4096,256]{1,0:T(8,128)(2,1)} %dout_ref.3), custom_call_target="tpu_custom_call" | custom-call | flops 49999998976 | bytes 20000000 | tf_op jit(solution)/shard_map/scatter/pallas_call | solution.py:554
  83.6 0.0 collective-permute-done.1.refs_4_
  83.6 0.0 copy-start.8
  83.6 0.0 collective-permute-done.11.refs_14_
  83.6 0.0 copy-start.9
  83.6 0.0 collective-permute-done.8.refs_11_
  83.6 0.0 collective-permute-done.5.refs_8_
  83.6 0.0 collective-permute-done.2.refs_5_
  83.7 0.7 copy-done.8
  84.4 0.2 copy-done.9
  84.6 335.2 %experts.1 = (bf16[64,224,512]{2,1,0:T(8,128)(2,1)}, f32[4,256,256]{2,1,0:T(8,128)}, f32[4,256,256]{2,1,0:T(8,128)}, f32[4,256,256]{2,1,0:T(8,128)}, f32[4,256,2...) custom-call(bf16[64,224,512]{2,1,0:T(8,128)(2,1)} %bitcast.15, ...), custom_call_target="tpu_custom_call" | custom-call | flops 299999985664 | bytes 60000000 | tf_op jit(solution)/shard_map/experts/pallas_call | solution.py:578
  419.8 1.5 collective-permute-start.14
  421.3 0.6 collective-permute-start.15
  421.9 0.6 collective-permute-start.12
  422.5 1.4 collective-permute-start.13
  423.9 44.9 %combine.1 = (bf16[4096,256]{1,0:T(8,128)(2,1)}, bf16[4096,256]{1,0:T(8,128)(2,1)}, f32[64,256]{1,0:T(8,128)}, f32[1,1]{1,0:T(1,128)}) custom-call(s32[32,2,128]{2,1,0:T(2,128)} %bitcast.17, bf16[14336,512]{1,0:T(8,128)(2,1)} %bitcast.14, f32[16,8,128]{2,1,0:T(8,128)} %get-tuple-element.44.tab_ref, f32[64,256]{1,0:T(8,128)} %bitcast.11, ...), custom_call_target="tpu_custom_call" | custom-call | flops 60000002048 | bytes 30000000 | tf_op jit(solution)/shard_map/combine/pallas_call | solution.py:614
  468.8 21.2 %collective-permute-done.12.refs_6_ = f32[8,256,256]{2,1,0:T(8,128)} collective-permute-done((f32[8,256,256]{2,1,0:T(8,128)}, f32[8,256,256]{2,1,0:T(8,128)}, u32[]{:S(2)}, u32[]{:S(2)}) %collective-permute-start.12) | collective-permute-done | bytes 2097184 | tf_op jit(solution)/shard_map/ppermute | solution.py:609
  490.0 1.1 collective-permute-done.13.refs_7_
  491.0 8.2 %place.1 = (f32[16,256,256]{2,1,0:T(8,128)}, f32[16,256,256]{2,1,0:T(8,128)}, f32[16,256,256]{2,1,0:T(8,128)}) custom-call(f32[4,256,256]{2,1,0:T(8,128)} %get-tuple-element.49.refs_0_, f32[4,256,256]{2,1,0:T(8,128)} %get-tuple-element.50.refs_1_, f32[4,256,256]{2,1,0:T(8,128)} %get-tuple-element.51.refs_2_, f32[4,256,256]{2,1,0:T(8,128)} %get-tuple-element.52.refs_3_, ...), custom_call_target="tpu_custom_call" | custom-call | flops 10000000000 | bytes 20000000 | tf_op jit(solution)/shard_map/place/pallas_call | solution.py:639
  499.3 9.6 %sum_router.1 = f32[64,256]{1,0:T(8,128)} custom-call(f32[64,256]{1,0:T(8,128)} %get-tuple-element.60.part_ref), custom_call_target="tpu_custom_call" | custom-call | flops 10000000000 | bytes 100000 | tf_op jit(solution)/shard_map/sum_router/pallas_call | solution.py:650
  508.8 0.0 copy-start.7
  508.8 0.0 collective-permute-done.14.first_ref
  508.9 0.0 collective-permute-done.15.second_ref
  508.9 1.4 place_last.1
  510.2 0.0 copy-done.7
  510.2 0.6 copy.17
Async XLA Ops:
  0.6 7.1 %copy-start = (bf16[16,256,256]{2,1,0:T(8,128)(2,1)S(1)}, bf16[16,256,256]{2,1,0:T(8,128)(2,1)}, u32[]{:S(2)}) copy-start(bf16[16,256,256]{2,1,0:T(8,128)(2,1)} %refs_0_.1) | copy-start | bytes 6291460
  2.9 16.4 %collective-permute-start = (bf16[4,256,256]{2,1,0:T(8,128)(2,1)}, bf16[4,256,256]{2,1,0:T(8,128)(2,1)}, u32[]{:S(2)}, u32[]{:S(2)}) collective-permute-start(bf16[4,256,256]{2,1,0:T(8,128)(2,1)} %get-tuple-element.40), channel_id=1, source_target_pairs={{0,8},{4,12},{8,0},{12,4},{1,9},{5,13},{9,1},{13,5},{2,10},{6,14},... | collective-permute-start | bytes 1572872 | tf_op jit(solution)/shard_map/ppermute | solution.py:523
  6.2 15.1 %collective-permute-start.3 = (bf16[4,256,256]{2,1,0:T(8,128)(2,1)S(1)}, bf16[4,256,256]{2,1,0:T(8,128)(2,1)}, u32[]{:S(2)}, u32[]{:S(2)}) collective-permute-start(bf16[4,256,256]{2,1,0:T(8,128)(2,1)S(1)} %get-tuple-element.41), channel_id=1, source_target_pairs={{0,4},{4,0},{8,12},{12,8},{1,5},{5,1},{9,13},{13,9},{2,6},{6,2},{1... | collective-permute-start | bytes 1572872 | tf_op jit(solution)/shard_map/ppermute | solution.py:524
  7.7 1.8 copy-start.1
  8.5 21.9 %collective-permute-start.9 = (bf16[4,256,256]{2,1,0:T(8,128)(2,1)}, bf16[4,256,256]{2,1,0:T(8,128)(2,1)}, u32[]{:S(2)}, u32[]{:S(2)}) collective-permute-start(bf16[4,256,256]{2,1,0:T(8,128)(2,1)} %get-tuple-element.75), channel_id=1, source_target_pairs={{0,8},{4,12},{8,0},{12,4},{1,9},{5,13},{9,1},{13,5},{2,10},{6,14},... | collective-permute-start | bytes 1572872 | tf_op jit(solution)/shard_map/ppermute | solution.py:526
  9.0 13.6 %copy-start.2 = (bf16[16,256,256]{2,1,0:T(8,128)(2,1)S(1)}, bf16[16,256,256]{2,1,0:T(8,128)(2,1)}, u32[]{:S(2)}) copy-start(bf16[16,256,256]{2,1,0:T(8,128)(2,1)} %refs_2_.1) | copy-start | bytes 6291460
  9.0 23.5 %collective-permute-start.6 = (bf16[4,256,256]{2,1,0:T(8,128)(2,1)S(1)}, bf16[4,256,256]{2,1,0:T(8,128)(2,1)}, u32[]{:S(2)}, u32[]{:S(2)}) collective-permute-start(bf16[4,256,256]{2,1,0:T(8,128)(2,1)S(1)} %get-tuple-element.76), channel_id=1, source_target_pairs={{0,4},{4,0},{8,12},{12,8},{1,5},{5,1},{9,13},{13,9},{2,6},{6,2},{1... | collective-permute-start | bytes 1572872 | tf_op jit(solution)/shard_map/ppermute | solution.py:525
  10.8 30.9 %collective-permute-start.10 = (bf16[4,256,256]{2,1,0:T(8,128)(2,1)}, bf16[4,256,256]{2,1,0:T(8,128)(2,1)}, u32[]{:S(2)}, u32[]{:S(2)}) collective-permute-start(bf16[4,256,256]{2,1,0:T(8,128)(2,1)} %get-tuple-element.71), channel_id=1, source_target_pairs={{0,8},{4,12},{8,0},{12,4},{1,9},{5,13},{9,1},{13,5},{2,10},{6,14},... | collective-permute-start | bytes 1572872 | tf_op jit(solution)/shard_map/ppermute | solution.py:526
  19.2 24.4 %collective-permute-start.7 = (bf16[4,256,256]{2,1,0:T(8,128)(2,1)}, bf16[4,256,256]{2,1,0:T(8,128)(2,1)}, u32[]{:S(2)}, u32[]{:S(2)}) collective-permute-start(bf16[4,256,256]{2,1,0:T(8,128)(2,1)} %get-tuple-element.72), channel_id=1, source_target_pairs={{0,4},{4,0},{8,12},{12,8},{1,5},{5,1},{9,13},{13,9},{2,6},{6,2},{1... | collective-permute-start | bytes 1572872 | tf_op jit(solution)/shard_map/ppermute | solution.py:525
  21.2 33.5 %collective-permute-start.4 = (bf16[4,256,256]{2,1,0:T(8,128)(2,1)}, bf16[4,256,256]{2,1,0:T(8,128)(2,1)}, u32[]{:S(2)}, u32[]{:S(2)}) collective-permute-start(bf16[4,256,256]{2,1,0:T(8,128)(2,1)} %get-tuple-element.73), channel_id=1, source_target_pairs={{0,4},{4,0},{8,12},{12,8},{1,5},{5,1},{9,13},{13,9},{2,6},{6,2},{1... | collective-permute-start | bytes 1572872 | tf_op jit(solution)/shard_map/ppermute | solution.py:524
  23.8 6.7 %copy-start.3 = (bf16[4,256,256]{2,1,0:T(8,128)(2,1)S(1)}, bf16[4,256,256]{2,1,0:T(8,128)(2,1)}, u32[]{:S(2)}) copy-start(bf16[4,256,256]{2,1,0:T(8,128)(2,1)} %get-tuple-element.74) | copy-start | bytes 1572868
  23.8 8.7 %copy-start.6 = (bf16[4,256,256]{2,1,0:T(8,128)(2,1)S(1)}, bf16[4,256,256]{2,1,0:T(8,128)(2,1)}, u32[]{:S(2)}) copy-start(bf16[4,256,256]{2,1,0:T(8,128)(2,1)} %get-tuple-element.67) | copy-start | bytes 1572868
  23.8 18.0 %copy-start.5 = (bf16[4,256,256]{2,1,0:T(8,128)(2,1)S(1)}, bf16[4,256,256]{2,1,0:T(8,128)(2,1)}, u32[]{:S(2)}) copy-start(bf16[4,256,256]{2,1,0:T(8,128)(2,1)} %get-tuple-element.68) | copy-start | bytes 1572868
  23.8 19.9 %copy-start.4 = (bf16[4,256,256]{2,1,0:T(8,128)(2,1)S(1)}, bf16[4,256,256]{2,1,0:T(8,128)(2,1)}, u32[]{:S(2)}) copy-start(bf16[4,256,256]{2,1,0:T(8,128)(2,1)} %get-tuple-element.69) | copy-start | bytes 1572868
  30.5 53.1 %collective-permute-start.1 = (bf16[4,256,256]{2,1,0:T(8,128)(2,1)S(1)}, bf16[4,256,256]{2,1,0:T(8,128)(2,1)S(1)}, u32[]{:S(2)}, u32[]{:S(2)}) collective-permute-start(bf16[4,256,256]{2,1,0:T(8,128)(2,1)S(1)} %copy-done.3), channel_id=1, source_target_pairs={{0,8},{4,12},{8,0},{12,4},{1,9},{5,13},{9,1},{13,5},{2,10},{6,14},... | collective-permute-start | bytes 1572872 | tf_op jit(solution)/shard_map/ppermute | solution.py:523
  32.5 51.1 %collective-permute-start.11 = (bf16[4,256,256]{2,1,0:T(8,128)(2,1)S(1)}, bf16[4,256,256]{2,1,0:T(8,128)(2,1)S(1)}, u32[]{:S(2)}, u32[]{:S(2)}) collective-permute-start(bf16[4,256,256]{2,1,0:T(8,128)(2,1)S(1)} %copy-done.6), channel_id=1, source_target_pairs={{0,8},{4,12},{8,0},{12,4},{1,9},{5,13},{9,1},{13,5},{2,10},{6,14},... | collective-permute-start | bytes 1572872 | tf_op jit(solution)/shard_map/ppermute | solution.py:526
  41.7 41.9 %collective-permute-start.8 = (bf16[4,256,256]{2,1,0:T(8,128)(2,1)S(1)}, bf16[4,256,256]{2,1,0:T(8,128)(2,1)}, u32[]{:S(2)}, u32[]{:S(2)}) collective-permute-start(bf16[4,256,256]{2,1,0:T(8,128)(2,1)S(1)} %copy-done.5), channel_id=1, source_target_pairs={{0,4},{4,0},{8,12},{12,8},{1,5},{5,1},{9,13},{13,9},{2,6},{6,2},{1... | collective-permute-start | bytes 1572872 | tf_op jit(solution)/shard_map/ppermute | solution.py:525
  43.7 39.9 %collective-permute-start.5 = (bf16[4,256,256]{2,1,0:T(8,128)(2,1)S(1)}, bf16[4,256,256]{2,1,0:T(8,128)(2,1)}, u32[]{:S(2)}, u32[]{:S(2)}) collective-permute-start(bf16[4,256,256]{2,1,0:T(8,128)(2,1)S(1)} %copy-done.4), channel_id=1, source_target_pairs={{0,4},{4,0},{8,12},{12,8},{1,5},{5,1},{9,13},{13,9},{2,6},{6,2},{1... | collective-permute-start | bytes 1572872 | tf_op jit(solution)/shard_map/ppermute | solution.py:524
  54.8 28.9 %collective-permute-start.2 = (bf16[4,256,256]{2,1,0:T(8,128)(2,1)S(1)}, bf16[4,256,256]{2,1,0:T(8,128)(2,1)}, u32[]{:S(2)}, u32[]{:S(2)}) collective-permute-start(bf16[4,256,256]{2,1,0:T(8,128)(2,1)S(1)} %get-tuple-element.70), channel_id=1, source_target_pairs={{0,8},{4,12},{8,0},{12,4},{1,9},{5,13},{9,1},{13,5},{2,10},{6,14},... | collective-permute-start | bytes 1572872 | tf_op jit(solution)/shard_map/ppermute | solution.py:523
  83.6 0.8 copy-start.8
  83.6 1.0 copy-start.9
  419.8 89.1 %collective-permute-start.14 = (f32[4,256,256]{2,1,0:T(8,128)}, f32[4,256,256]{2,1,0:T(8,128)S(1)}, u32[]{:S(2)}, u32[]{:S(2)}) collective-permute-start(f32[4,256,256]{2,1,0:T(8,128)} %get-tuple-element.64), channel_id=1, source_target_pairs={{0,8},{4,12},{8,0},{12,4},{1,9},{5,13},{9,1},{13,5},{2,10},{6,14},... | collective-permute-start | bytes 3145736 | tf_op jit(solution)/shard_map/ppermute | solution.py:610
  421.3 87.6 %collective-permute-start.15 = (f32[4,256,256]{2,1,0:T(8,128)}, f32[4,256,256]{2,1,0:T(8,128)S(1)}, u32[]{:S(2)}, u32[]{:S(2)}) collective-permute-start(f32[4,256,256]{2,1,0:T(8,128)} %get-tuple-element.65), channel_id=1, source_target_pairs={{0,4},{4,0},{8,12},{12,8},{1,5},{5,1},{9,13},{13,9},{2,6},{6,2},{1... | collective-permute-start | bytes 3145736 | tf_op jit(solution)/shard_map/ppermute | solution.py:610
  421.9 68.1 %collective-permute-start.12 = (f32[8,256,256]{2,1,0:T(8,128)}, f32[8,256,256]{2,1,0:T(8,128)}, u32[]{:S(2)}, u32[]{:S(2)}) collective-permute-start(f32[8,256,256]{2,1,0:T(8,128)} %get-tuple-element.55), channel_id=1, source_target_pairs={{0,8},{4,12},{8,0},{12,4},{1,9},{5,13},{9,1},{13,5},{2,10},{6,14},... | collective-permute-start | bytes 6291464 | tf_op jit(solution)/shard_map/ppermute | solution.py:609
  422.5 68.6 %collective-permute-start.13 = (f32[8,256,256]{2,1,0:T(8,128)}, f32[8,256,256]{2,1,0:T(8,128)}, u32[]{:S(2)}, u32[]{:S(2)}) collective-permute-start(f32[8,256,256]{2,1,0:T(8,128)} %get-tuple-element.56), channel_id=1, source_target_pairs={{0,4},{4,0},{8,12},{12,8},{1,5},{5,1},{9,13},{13,9},{2,6},{6,2},{1... | collective-permute-start | bytes 6291464 | tf_op jit(solution)/shard_map/ppermute | solution.py:609
  508.8 1.4 copy-start.7
